TPU v7x, 256 devices: a whole 4x4x8 slice. The times are simulated.
256 devices in a mesh: rp: 8 (over x, z_lo), pb: 32 (over z_hi, y, core).
Axes of the slice: x: 4, y: 4, z: 8 (z_hi: 4, z_lo: 2; z = z_hi * 2 + z_lo), core: 2. Of those that a mesh axis runs over, the one named last changes fastest.
Arguments:
- wannier_g: bfloat16 [2, 1024, 32, 1152], P(None, 'rp', 'pb'), may hold values from -0.19921875 to 0.19921875
- rp_coords: int32 [3, 1024], replicated, may hold values from -8 to 8
- q_coords: int32 [3, 512], P(None, ('rp', 'pb')), may hold values from 0 to 15
- k_index: int32 [1], replicated, may hold values from 0 to 7
- k_vectors: bfloat16 [8, 2, 32, 32], replicated, may hold values from -0.75 to 0.75
- kq_vectors: bfloat16 [512, 2, 32, 32], P(('rp', 'pb')), may hold values from -0.75 to 0.75
- modes: bfloat16 [512, 2, 36, 36], P(('rp', 'pb')), may hold values from -0.75 to 0.75
Outputs:
- rotated: float32 [512, 2, 32, 1152], P(('rp', 'pb'))
All inputs are finite; a program needn't handle non-finite values.
Results may differ from a plain program's by a relative error of at most 0.0054.
Values may be sent and summed in bfloat16 or wider, within the bound.
A program may use at most 64 MiB of HBM per device.

v0:
```python
import math
import jax
import jax.numpy as jnp
from jax import lax
from jax.sharding import PartitionSpec as P

NK = 16


def in_blocks(x, dim, length):
    shape = x.shape
    parts = x.reshape(*shape[:dim], length, shape[dim] // length, *shape[dim + 1 :])
    return jnp.moveaxis(parts, dim, 0)


def joined_along(parts, dim):
    shape = list(parts.shape[1:])
    shape[dim] *= parts.shape[0]
    return jnp.moveaxis(parts, 0, dim).reshape(shape)


def one_exchange(x, axis, axes, splits, concats):
    sizes = [lax.axis_size(a) for a in axes]
    parts = in_blocks(x, splits[0], sizes[0])
    parts = jnp.moveaxis(in_blocks(parts, splits[1] + 1, sizes[1]), 0, 1)
    inside = parts.shape[2:]
    parts = parts.reshape(-1, *inside)
    parts = lax.all_to_all(parts, axis, split_axis=0, concat_axis=0, tiled=True)
    parts = joined_along(parts.reshape(*sizes, *inside), concats[0] + 1)
    return joined_along(parts, concats[1])


def phases(q_rows, r_coords):
    turns = jnp.mod(jnp.sum(q_rows[:, :, None] * r_coords[:, None, :], axis=0), NK)
    angle = turns.astype(jnp.float32) * (2.0 * math.pi / NK)
    cosine = jnp.cos(angle).astype(jnp.bfloat16)
    sine = jnp.sin(angle).astype(jnp.bfloat16)
    return (jnp.concatenate([cosine, -sine], axis=1), jnp.concatenate([sine, cosine], axis=1))


def rotate(fourier, mode_vecs, unit, kq_vecs):
    count = fourier.shape[0]
    bands = kq_vecs.shape[2]
    branches = mode_vecs.shape[2]
    field = fourier.reshape(count, 2, bands, bands, branches)
    e_real, e_imag = (mode_vecs[:, 0], mode_vecs[:, 1])
    e_block = jnp.stack([jnp.stack([e_real, e_imag], 2), jnp.stack([-e_imag, e_real], 2)], 1)
    by_mode = jnp.einsum(
        "qcmnv,qcvdu->qdmnu", field, e_block, preferred_element_type=jnp.float32
    ).astype(jnp.bfloat16)
    u_real, u_imag = (unit[0], unit[1])
    u_block = jnp.stack([jnp.stack([u_real, u_imag], 1), jnp.stack([-u_imag, u_real], 1)], 0)
    by_band = jnp.einsum(
        "qcmnu,cndj->qdmju", by_mode, u_block, preferred_element_type=jnp.float32
    ).astype(jnp.bfloat16)
    v_real, v_imag = (kq_vecs[:, 0], kq_vecs[:, 1])
    v_block = jnp.stack([jnp.stack([v_real, -v_imag], 2), jnp.stack([v_imag, v_real], 2)], 1)
    result = jnp.einsum("qcmju,qcmdi->qdiju", by_band, v_block, preferred_element_type=jnp.float32)
    return result.reshape(count, 2, bands, bands * branches)


def local(wannier_g, rp_coords, q_coords, k_index, k_vectors, kq_vectors, modes):
    q_all = lax.all_gather(q_coords, ("rp", "pb"), axis=1, tiled=True)
    total = q_all.shape[1]
    groups = lax.axis_size("rp")
    block = total // groups
    moved = lax.all_to_all(wannier_g, "rp", split_axis=3, concat_axis=1, tiled=True)
    right = moved.reshape(2 * moved.shape[1], -1)
    q_blocks = q_all.reshape(3, groups, block).transpose(1, 0, 2)

    def fourier_block(q_rows):
        left_real, left_imag = phases(q_rows, rp_coords)
        f_real = jnp.dot(left_real, right, preferred_element_type=jnp.float32).astype(jnp.bfloat16)
        f_imag = jnp.dot(left_imag, right, preferred_element_type=jnp.float32).astype(jnp.bfloat16)
        return jnp.stack([f_real, f_imag], 1)

    fourier = lax.map(fourier_block, q_blocks).reshape(total, 2, moved.shape[2], moved.shape[3])
    owned = one_exchange(fourier, ("rp", "pb"), ("rp", "pb"), (0, 0), (3, 2))
    select = (jnp.arange(k_vectors.shape[0]) == k_index[0]).astype(jnp.bfloat16)
    unit = jnp.einsum("k,kcnj->cnj", select, k_vectors, preferred_element_type=jnp.float32).astype(
        jnp.bfloat16
    )
    return rotate(owned, modes, unit, kq_vectors)


def solution(mesh):
    return jax.shard_map(
        local,
        mesh=mesh,
        in_specs=(
            P(None, "rp", "pb", None),
            P(),
            P(None, ("rp", "pb")),
            P(),
            P(),
            P(("rp", "pb"), None, None, None),
            P(("rp", "pb"), None, None, None),
        ),
        out_specs=P(("rp", "pb"), None, None, None),
        check_vma=False,
    )
```

profile of v0, /device:TPU:1, one launch (start us, length us, event | category | flops | bytes accessed | tf_op | source)
XLA Modules:
  0.0 424.2 jit_solution(9630580377085636037)
XLA Ops:
  0.0 3.0 copy.101
  3.0 6.2 %all-to-all-start = ((bf16[2,128,1,1152]{1,0,2,3:T(2,128)(2,1)}), bf16[2,128,1,1152]{1,0,2,3:T(2,128)(2,1)S(1)}, u32[]{:S(2)}, u32[]{:S(2)}) async-start(bf16[2,128,1,1152]{1,0,2,3:T(2,128)(2,1)} %copy.101), calls=%async_computation | async-start | bytes 1179648 | tf_op jit(solution)/shard_map/all_to_all | solution.py:67
  10.3 350.8 %all-gather = s32[256,2,3]{2,1,0:T(2,128)S(1)} all-gather(s32[1,2,3]{2,1,0:T(2,128)S(1)} %bitcast.145), channel_id=1, replica_groups=mesh['rp'=8,'pb'=32] {'rp','pb'}, dimensions={0}, use_global_device_ids=true | all-gather | bytes 6168 | tf_op jit(solution)/shard_map/all_gather | solution.py:63
  361.4 0.5 copy.128
  362.0 27.2 %while.12 = (s32[]{:T(128)}, bf16[8,64,2,144]{3,2,1,0:T(2,128)(2,1)}, s32[8,3,64]{2,0,1:T(8,128)S(1)}, s32[3,1024]{1,0:T(4,128)S(1)}, bf16[2048,144]{1,0:T(8,128)(2,1)S(1)}, /*index=5*/s32[]{:T(128)}) while((s32[]{:T(128)}, bf16[8,64,2,144]{3,2,1,0:T(2,128)(2,1)}, s32[8,3,64]{2,0,1:T(8,128)S(1)}, s32[3,1024]{1,0:T(4,128)S(1)}, ...), condition=%wide.region_2.3_spmd, body=%wide.region_0.2_spmd.sunk | while | flops 78942208 | bytes 3112789 | solution.py:77
  362.1 0.9 cosine_convert_fusion.2
  363.1 1.0 fusion.51
  364.4 0.3 fusion.53
  364.7 0.7 copy_dynamic-update-slice_fusion.2
  365.5 0.9 cosine_convert_fusion.2
  366.5 1.0 fusion.51
  367.4 0.3 fusion.52
  368.1 0.7 copy_dynamic-update-slice_fusion.2
  368.9 0.9 cosine_convert_fusion.2
  369.9 1.0 fusion.51
  371.1 0.3 fusion.53
  371.5 0.7 copy_dynamic-update-slice_fusion.2
  372.3 0.9 cosine_convert_fusion.2
  373.3 1.0 fusion.51
  374.9 0.7 copy_dynamic-update-slice_fusion.2
  375.7 0.9 cosine_convert_fusion.2
  376.6 1.0 fusion.51
  377.6 0.3 fusion.52
  377.9 0.3 fusion.53
  378.2 0.7 copy_dynamic-update-slice_fusion.2
  379.1 0.9 cosine_convert_fusion.2
  380.0 1.0 fusion.51
  381.3 0.3 fusion.53
  381.6 0.7 copy_dynamic-update-slice_fusion.2
  382.5 0.9 cosine_convert_fusion.2
  383.4 1.0 fusion.51
  384.4 0.3 fusion.52
  384.7 0.3 fusion.53
  385.0 0.7 copy_dynamic-update-slice_fusion.2
  385.9 0.9 cosine_convert_fusion.2
  386.8 1.0 fusion.51
  387.8 0.3 fusion.52
  388.4 0.7 copy_dynamic-update-slice_fusion.2
  389.1 5.3 %all-to-all-start.1 = ((bf16[256,2,2,1,144]{4,2,1,3,0:T(2,128)(2,1)}), bf16[256,2,2,1,144]{4,2,1,3,0:T(2,128)(2,1)S(1)}, u32[]{:S(2)}, u32[]{:S(2)}) async-start(bf16[256,2,2,1,144]{4,2,1,3,0:T(2,128)(2,1)} %bitcast.38), calls=%async_computation.1 | async-start | bytes 1048576 | tf_op jit(solution)/shard_map/all_to_all | solution.py:28
  394.9 20.4 %all-to-all-done.1 = bf16[256,2,2,1,144]{4,2,1,3,0:T(2,128)(2,1)S(1)} async-done(((bf16[256,2,2,1,144]{4,2,1,3,0:T(2,128)(2,1)}), bf16[256,2,2,1,144]{4,2,1,3,0:T(2,128)(2,1)S(1)}, u32[]{:S(2)}, u32[]{:S(2)}) %all-to-all-start.1) | async-done | bytes 294944 | tf_op jit(solution)/shard_map/all_to_all | solution.py:28
  415.4 0.3 copy.109
  415.7 0.5 reshape.52
  416.2 2.8 reshape_reshape.3
  419.0 0.5 fusion.13
  419.5 0.5 fusion.14
  420.0 0.5 convolution_bitcast_fusion
  420.5 1.2 copy.114
  421.7 2.4 reshape.53
  (70 shorter events, 4.5 us)
Async XLA Ops:
  0.0 9.9 %copy-start = (bf16[8,2,32,32]{3,2,1,0:T(8,128)(2,1)S(1)}, bf16[8,2,32,32]{3,2,1,0:T(8,128)(2,1)}, u32[]{:S(2)}) copy-start(bf16[8,2,32,32]{3,2,1,0:T(8,128)(2,1)} %param.13) | copy-start | bytes 98308
  0.0 10.2 %copy-start.3 = (bf16[2,2,32,32]{3,2,1,0:T(8,128)(2,1)S(1)}, bf16[2,2,32,32]{3,2,1,0:T(8,128)(2,1)}, u32[]{:S(2)}) copy-start(bf16[2,2,32,32]{3,2,1,0:T(8,128)(2,1)} %param.14) | copy-start | bytes 24580
  0.0 10.3 %copy-start.4 = (s32[3,2]{0,1:T(2,128)S(1)}, s32[3,2]{0,1:T(2,128)}, u32[]{:S(2)}) copy-start(s32[3,2]{0,1:T(2,128)} %param.11) | copy-start | bytes 76
  0.0 361.3 %copy-start.2 = (bf16[2,2,36,36]{3,1,2,0:T(2,128)(2,1)S(1)}, bf16[2,2,36,36]{3,1,2,0:T(2,128)(2,1)}, u32[]{:S(2)}) copy-start(bf16[2,2,36,36]{3,1,2,0:T(2,128)(2,1)} %param.15) | copy-start | bytes 31108
  3.0 358.3 %all-to-all-start = ((bf16[2,128,1,1152]{1,0,2,3:T(2,128)(2,1)}), bf16[2,128,1,1152]{1,0,2,3:T(2,128)(2,1)S(1)}, u32[]{:S(2)}, u32[]{:S(2)}) async-start(bf16[2,128,1,1152]{1,0,2,3:T(2,128)(2,1)} %copy.101), calls=%async_computation | async-start | bytes 1179648 | tf_op jit(solution)/shard_map/all_to_all | solution.py:67
  9.2 352.8 %copy-start.1 = (s32[3,1024]{1,0:T(4,128)S(1)}, s32[3,1024]{1,0:T(4,128)}, u32[]{:S(2)}) copy-start(s32[3,1024]{1,0:T(4,128)} %param.10) | copy-start | bytes 36868
  389.1 26.2 %all-to-all-start.1 = ((bf16[256,2,2,1,144]{4,2,1,3,0:T(2,128)(2,1)}), bf16[256,2,2,1,144]{4,2,1,3,0:T(2,128)(2,1)S(1)}, u32[]{:S(2)}, u32[]{:S(2)}) async-start(bf16[256,2,2,1,144]{4,2,1,3,0:T(2,128)(2,1)} %bitcast.38), calls=%async_computation.1 | async-start | bytes 1048576 | tf_op jit(solution)/shard_map/all_to_all | solution.py:28
where the time goes:
time: 424 us
  blocking collectives  351 us (83%)
  waiting for transfers between devices  20.4 us (5%)
  local copies, waits for them, and re-layouts  17 us (4%)
  other arithmetic  16.8 us (4%)
  starting transfers between devices  11.5 us (3%)
  matrix products  6.36 us (2%)
    all_gather x1, blocking collectives, local(): q_all = lax.all_gather(q_coords, ('rp', 'pb'), axis=1, tiled=True)  351 us
    all_to_all x1, waiting for transfers between devices, one_exchange(): parts = lax.all_to_all(parts, axis, split_axis=0, concat_axis=0, tiled=True)  20.4 us
  transfers between devices with their start and end apart: 2, of which 1 were waited for; matrix products, arithmetic and copies ran while one was open for 0% of the time, Pallas kernels for 0%

commit v1 on v0

--- a/solution.py
+++ b/solution.py
@@ -60,7 +60,10 @@
 
 
 def local(wannier_g, rp_coords, q_coords, k_index, k_vectors, kq_vectors, modes):
-    q_all = lax.all_gather(q_coords, ("rp", "pb"), axis=1, tiled=True)
+    q_all = jnp.concatenate(
+        lax.all_to_all(jnp.stack(lax.axis_size(("rp", "pb")) * [q_coords], 0), ("rp", "pb"), 0, 0),
+        1,
+    )
     total = q_all.shape[1]
     groups = lax.axis_size("rp")
     block = total // groups

time: 424 us -> 111 us (0.26)
  blocking collectives: 351 us -> 0 us
  waiting for transfers between devices: 20.4 us -> 42 us
  starting transfers between devices: 11.5 us -> 25.8 us
    all_gather x1 -> x0, blocking collectives: 351 us -> none  [local(): q_all = lax.all_gather(q_coords, ('rp', 'pb'), axis=1, tiled=True)]
    all_to_all x0 -> x1, starting transfers between devices: none -> 15.6 us  [local(): lax.all_to_all(jnp.stack(lax.axis_size(('rp', 'pb')) * [q_coords], 0), ('...]
    all_to_all x0 -> x1, waiting for transfers between devices: none -> 11.7 us  [local(): lax.all_to_all(jnp.stack(lax.axis_size(('rp', 'pb')) * [q_coords], 0), ('...]
    all_to_all x1, waiting for transfers between devices: 0.01 us -> 9.78 us  [local(): lax.all_to_all(wannier_g, 'rp', split_axis=3, concat_axis=1, tiled=True)]
  transfers between devices with their start and end apart: 2 -> 3, of which waited for: 1 -> 3; matrix products, arithmetic and copies ran while one was open for 0% -> 4% of each run, Pallas kernels for 0% -> 0%
where the time goes in v1:
time: 111 us
  waiting for transfers between devices  42 us (38%)
  starting transfers between devices  25.8 us (23%)
  local copies, waits for them, and re-layouts  18.4 us (17%)
  other arithmetic  16.8 us (15%)
  matrix products  6.36 us (6%)
    all_to_all x1, waiting for transfers between devices, one_exchange(): parts = lax.all_to_all(parts, axis, split_axis=0, concat_axis=0, tiled=True)  20.6 us
    all_to_all x1, starting transfers between devices, local(): lax.all_to_all(jnp.stack(lax.axis_size(('rp', 'pb')) * [q_coords], 0), ('...  15.6 us
    all_to_all x1, waiting for transfers between devices, local(): lax.all_to_all(jnp.stack(lax.axis_size(('rp', 'pb')) * [q_coords], 0), ('...  11.7 us
    all_to_all x1, waiting for transfers between devices, local(): lax.all_to_all(wannier_g, 'rp', split_axis=3, concat_axis=1, tiled=True)  9.78 us
    neg x8, other arithmetic, phases(): -sine  7.76 us
    convert_element_type x8, other arithmetic, phases(): cosine = jnp.cos(angle).astype(jnp.bfloat16)  7.6 us
    all_to_all x1, starting transfers between devices, one_exchange(): parts = lax.all_to_all(parts, axis, split_axis=0, concat_axis=0, tiled=True)  6.58 us
    dynamic_update_slice x8, local copies, waits for them, and re-layouts, local(): lax.map(fourier_block, q_blocks)  5.58 us
  transfers between devices with their start and end apart: 3, of which 3 were waited for; matrix products, arithmetic and copies ran while one was open for 4% of the time, Pallas kernels for 0%

profile of v1, /device:TPU:1, one launch (start us, length us, event | category | flops | bytes accessed | tf_op | source)
XLA Modules:
  0.0 110.6 jit_solution(1078761208489852443)
XLA Ops:
  0.0 1.5 %stack.62 = s32[256,3,2]{1,2,0:T(2,128)} broadcast(s32[3,2]{0,1:T(2,128)} %param.11), dimensions={1,2} | broadcast | bytes 6168 | tf_op jit(solution)/shard_map/stack | solution.py:64
  1.5 15.6 %all-to-all-start = ((s32[256,3,2]{1,2,0:T(2,128)}), s32[256,3,2]{1,2,0:T(2,128)S(1)}, u32[]{:S(2)}, u32[]{:S(2)}) async-start(s32[256,3,2]{1,2,0:T(2,128)} %stack.62), calls=%async_computation | async-start | bytes 524288 | tf_op jit(solution)/shard_map/all_to_all | solution.py:64
  18.1 2.9 %copy.102 = bf16[2,128,1,1152]{1,0,2,3:T(2,128)(2,1)} copy(bf16[2,128,1,1152]{3,1,2,0:T(8,128)(2,1)} %param.9) | data formatting | bytes 1179648 | tf_op args[0]
  21.1 11.7 %all-to-all-done = s32[256,3,2]{1,2,0:T(2,128)S(1)} async-done(((s32[256,3,2]{1,2,0:T(2,128)}), s32[256,3,2]{1,2,0:T(2,128)S(1)}, u32[]{:S(2)}, u32[]{:S(2)}) %all-to-all-start) | async-done | bytes 6176 | tf_op jit(solution)/shard_map/all_to_all | solution.py:64
  32.7 3.5 %all-to-all-start.1 = ((bf16[2,128,1,1152]{1,0,2,3:T(2,128)(2,1)}), bf16[2,128,1,1152]{1,0,2,3:T(2,128)(2,1)S(1)}, u32[]{:S(2)}, u32[]{:S(2)}) async-start(bf16[2,128,1,1152]{1,0,2,3:T(2,128)(2,1)} %copy.102), calls=%async_computation.1 | async-start | bytes 1179648 | tf_op jit(solution)/shard_map/all_to_all | solution.py:70
  36.6 9.8 %all-to-all-done.1 = bf16[2,128,1,1152]{1,0,2,3:T(2,128)(2,1)S(1)} async-done(((bf16[2,128,1,1152]{1,0,2,3:T(2,128)(2,1)}), bf16[2,128,1,1152]{1,0,2,3:T(2,128)(2,1)S(1)}, u32[]{:S(2)}, u32[]{:S(2)}) %all-to-all-start.1) | async-done | bytes 589856 | tf_op jit(solution)/shard_map/all_to_all | solution.py:70
  46.5 0.5 copy.131
  47.0 27.1 %while.12 = (s32[]{:T(128)}, bf16[8,64,2,144]{3,2,1,0:T(2,128)(2,1)}, s32[8,3,64]{2,1,0:T(4,128)S(1)}, s32[3,1024]{1,0:T(4,128)S(1)}, bf16[2048,144]{1,0:T(8,128)(2,1)S(1)}, /*index=5*/s32[]{:T(128)}) while((s32[]{:T(128)}, bf16[8,64,2,144]{3,2,1,0:T(2,128)(2,1)}, s32[8,3,64]{2,1,0:T(4,128)S(1)}, s32[3,1024]{1,0:T(4,128)S(1)}, ...), condition=%wide.region_2.3_spmd, body=%wide.region_0.2_spmd.sunk | while | flops 78942208 | bytes 3111253 | solution.py:80
  47.2 0.9 cosine_convert_fusion.2
  48.1 1.0 fusion.51
  49.7 0.7 copy_dynamic-update-slice_fusion.2
  50.5 0.9 cosine_convert_fusion.2
  51.5 1.0 fusion.51
  53.1 0.7 copy_dynamic-update-slice_fusion.2
  53.9 0.9 cosine_convert_fusion.2
  54.9 1.0 fusion.51
  56.1 0.3 fusion.53
  56.5 0.7 copy_dynamic-update-slice_fusion.2
  57.3 0.9 cosine_convert_fusion.2
  58.3 1.0 fusion.51
  59.2 0.3 fusion.52
  59.5 0.3 fusion.53
  59.9 0.7 copy_dynamic-update-slice_fusion.2
  60.7 0.9 cosine_convert_fusion.2
  61.6 1.0 fusion.51
  62.6 0.3 fusion.52
  62.9 0.3 fusion.53
  63.2 0.7 copy_dynamic-update-slice_fusion.2
  64.1 0.9 cosine_convert_fusion.2
  65.0 1.0 fusion.51
  66.6 0.7 copy_dynamic-update-slice_fusion.2
  67.5 0.9 cosine_convert_fusion.2
  68.4 1.0 fusion.51
  70.0 0.7 copy_dynamic-update-slice_fusion.2
  70.9 0.9 cosine_convert_fusion.2
  71.8 1.0 fusion.51
  73.1 0.3 fusion.53
  73.4 0.7 copy_dynamic-update-slice_fusion.2
  74.1 6.6 %all-to-all-start.2 = ((bf16[256,2,2,1,144]{4,2,1,3,0:T(2,128)(2,1)}), bf16[256,2,2,1,144]{4,2,1,3,0:T(2,128)(2,1)S(1)}, u32[]{:S(2)}, u32[]{:S(2)}) async-start(bf16[256,2,2,1,144]{4,2,1,3,0:T(2,128)(2,1)} %bitcast.37), calls=%async_computation.2 | async-start | bytes 1048576 | tf_op jit(solution)/shard_map/all_to_all | solution.py:28
  81.2 20.6 %all-to-all-done.2 = bf16[256,2,2,1,144]{4,2,1,3,0:T(2,128)(2,1)S(1)} async-done(((bf16[256,2,2,1,144]{4,2,1,3,0:T(2,128)(2,1)}), bf16[256,2,2,1,144]{4,2,1,3,0:T(2,128)(2,1)S(1)}, u32[]{:S(2)}, u32[]{:S(2)}) %all-to-all-start.2) | async-done | bytes 294944 | tf_op jit(solution)/shard_map/all_to_all | solution.py:28
  101.8 0.3 copy.110
  102.1 0.5 reshape.54
  102.6 2.8 %reshape_reshape.7 = bf16[2,2,32,32,36]{4,3,2,1,0:T(8,128)(2,1)S(1)} reshape(bf16[2,2,32,1,1152]{4,2,1,0,3:T(8,128)(2,1)S(1)} %bitcast.134) | data formatting | bytes 589824 | tf_op jit(solution)/shard_map/reshape;reshape | solution.py:45
  105.4 0.5 fusion.13
  105.9 0.5 fusion.14
  106.4 0.5 convolution_bitcast_fusion
  106.9 1.2 %copy.115 = f32[2,2,32,32,36]{4,3,2,1,0:T(8,128)S(1)} copy(f32[2,2,32,32,36]{4,2,3,1,0:T(8,128)S(1)} %convolution_bitcast_fusion) | data formatting | bytes 1179648 | tf_op jit(solution)/shard_map/qcmju,qcmdi->qdiju/dot_general | solution.py:58
  108.1 2.4 %reshape.55 = f32[2,2,32,1152]{3,2,1,0:T(8,128)} reshape(f32[2,2,32,32,36]{4,3,2,1,0:T(8,128)S(1)} %copy.115) | data formatting | bytes 1179648 | tf_op jit(solution)/shard_map/reshape | solution.py:59
  (61 shorter events, 5.2 us)
Async XLA Ops:
  0.0 17.8 %copy-start = (bf16[8,2,32,32]{3,2,1,0:T(8,128)(2,1)S(1)}, bf16[8,2,32,32]{3,2,1,0:T(8,128)(2,1)}, u32[]{:S(2)}) copy-start(bf16[8,2,32,32]{3,2,1,0:T(8,128)(2,1)} %param.13) | copy-start | bytes 98308
  0.0 36.3 %copy-start.3 = (bf16[2,2,32,32]{3,2,1,0:T(8,128)(2,1)S(1)}, bf16[2,2,32,32]{3,2,1,0:T(8,128)(2,1)}, u32[]{:S(2)}) copy-start(bf16[2,2,32,32]{3,2,1,0:T(8,128)(2,1)} %param.14) | copy-start | bytes 24580
  0.0 36.4 %copy-start.2 = (bf16[2,2,36,36]{3,1,2,0:T(2,128)(2,1)S(1)}, bf16[2,2,36,36]{3,1,2,0:T(2,128)(2,1)}, u32[]{:S(2)}) copy-start(bf16[2,2,36,36]{3,1,2,0:T(2,128)(2,1)} %param.15) | copy-start | bytes 31108
  1.5 31.2 %all-to-all-start = ((s32[256,3,2]{1,2,0:T(2,128)}), s32[256,3,2]{1,2,0:T(2,128)S(1)}, u32[]{:S(2)}, u32[]{:S(2)}) async-start(s32[256,3,2]{1,2,0:T(2,128)} %stack.62), calls=%async_computation | async-start | bytes 524288 | tf_op jit(solution)/shard_map/all_to_all | solution.py:64
  21.1 25.9 %copy-start.1 = (s32[3,1024]{1,0:T(4,128)S(1)}, s32[3,1024]{1,0:T(4,128)}, u32[]{:S(2)}) copy-start(s32[3,1024]{1,0:T(4,128)} %param.10) | copy-start | bytes 36868
  32.7 13.7 %all-to-all-start.1 = ((bf16[2,128,1,1152]{1,0,2,3:T(2,128)(2,1)}), bf16[2,128,1,1152]{1,0,2,3:T(2,128)(2,1)S(1)}, u32[]{:S(2)}, u32[]{:S(2)}) async-start(bf16[2,128,1,1152]{1,0,2,3:T(2,128)(2,1)} %copy.102), calls=%async_computation.1 | async-start | bytes 1179648 | tf_op jit(solution)/shard_map/all_to_all | solution.py:70
  74.1 27.6 %all-to-all-start.2 = ((bf16[256,2,2,1,144]{4,2,1,3,0:T(2,128)(2,1)}), bf16[256,2,2,1,144]{4,2,1,3,0:T(2,128)(2,1)S(1)}, u32[]{:S(2)}, u32[]{:S(2)}) async-start(bf16[256,2,2,1,144]{4,2,1,3,0:T(2,128)(2,1)} %bitcast.37), calls=%async_computation.2 | async-start | bytes 1048576 | tf_op jit(solution)/shard_map/all_to_all | solution.py:28
